TPU v7x, 256 devices: a whole 4x4x8 slice. The times are simulated.
256 devices in a mesh: kf: 64 (over z, y, core), kc: 4 (over x).
Axes of the slice: x: 4, y: 4, z: 8, core: 2. Of those that a mesh axis runs over, the one named last changes fastest.
Arguments:
- kernel_coarse: bfloat16 [2048, 2048], P('kf'), may hold values from -6 to 6
- coefficients: bfloat16 [1024, 256], P(('kf', 'kc')), may hold values from -1.5 to 1.5
- nearest: int32 [1024], replicated, may hold values from 0 to 127
Outputs:
- kernel_fine: bfloat16 [16384, 16384], P('kf', 'kc')
All inputs are finite; a program needn't handle non-finite values.
Results may differ from a plain program's by a relative error of at most 0.0049.
Values may be sent and summed in bfloat16 or wider, within the bound.
No kernel may reach another device: no remote copies, remote signals or barrier semaphores. Data moves between devices by JAX's collectives and lax.ppermute only.
A program may use at most 64 MiB of HBM per device.

v0:
```python
import jax
import jax.numpy as jnp
from jax import lax
from jax.experimental import pallas as pl
from jax.experimental.pallas import tpu as pltpu
from jax.sharding import Mesh
from jax.sharding import PartitionSpec as P


KF = ("kf_0", "kf_1", "kf_2")
ZY = ("kf_0", "kf_1")
KF_KC = ("kf_0", "kf_1", "kf_2", "kc")
LANES = 128
PAIRS = 16
POINTS = 4
PEERS = 32
FINE = 1024
BF16 = jnp.bfloat16
F32 = jnp.float32
VMEM = pl.BlockSpec(memory_space=pltpu.VMEM)
SMEM = pl.BlockSpec(memory_space=pltpu.SMEM)
ANY = pl.BlockSpec(memory_space=pl.ANY)


def iota(shape, dim):
    return lax.broadcasted_iota(jnp.int32, shape, dim)


def dot_t(a, b):
    return lax.dot_general(a, b, (((1,), (1,)), ((), ())), preferred_element_type=F32)


def turn_rows(rows, copies):
    for b in range(16):
        block = rows[:32, b * LANES : (b + 1) * LANES].astype(F32)
        for s in range(8):
            turned = pltpu.roll(block, s * PAIRS, 1) if s else block
            copies[s * 16 + b] = turned.astype(BF16)


def halves_stacked(coef):
    return jnp.concatenate([coef[:, :LANES], coef[:, LANES:]], axis=0)


def own_kernel(fetched, copies, near, slots, coef):
    c = fetched[32:33, :FINE].astype(jnp.int32)
    near[...] = c
    slots[...] = ((iota((1, FINE), 1) % POINTS - c) & 7) * 16 + (c >> 3)
    coef[...] = halves_stacked(fetched[40:44, : 2 * LANES]).astype(BF16)
    turn_rows(fetched, copies)


def index_copy(near, scalars, sem):
    return pltpu.make_async_copy(near, scalars, sem.at[0])


def pack_kernel(slots, own_copies, other, coef, out, other_copies, scalars, sem):
    fetch = index_copy(slots, scalars, sem)
    fetch.start()
    kc = lax.axis_index("kc")
    core = lax.axis_index("kf_2")
    turn_rows(other, other_copies)
    copies = (own_copies, other_copies)
    fetch.wait()
    group = iota((PAIRS, LANES), 1) // PAIRS
    base = 16 * core + 4 * kc

    def body(d, carry):
        tiles = [None, None]
        for j in range(POINTS):
            slot = scalars[0, 32 * d + base + j]
            for lo in range(2):
                for n in range(2):
                    piece = copies[n][slot ^ (64 * lo), lo * PAIRS : (lo + 1) * PAIRS, :]
                    tiles[n] = piece if tiles[n] is None else jnp.where(group == lo * POINTS + j, piece, tiles[n])
        out[d, pl.ds(pl.multiple_of(core * PAIRS, PAIRS), PAIRS), :] = tiles[0]
        out[d, pl.ds(pl.multiple_of((1 - core) * PAIRS, PAIRS), PAIRS), :] = tiles[1]
        out[d, 2 * PAIRS :, :] = coef[...]
        return carry

    lax.fori_loop(0, PEERS, body, 0, unroll=4)


def row_block(received, n):
    return received[n // 2, n % 2 * PAIRS : (n % 2 + 1) * PAIRS, :]


def row_coefficients(coef_own):
    mine = coef_own[...].astype(F32)
    return jnp.concatenate([mine, mine], axis=0).astype(BF16)


def put_pieces(received, kc, target, at):
    for p in range(8):
        target[at + p // 2, p % 2 * 8 : p % 2 * 8 + 8, :] = received[kc * 8 + p, 2 * PAIRS :, :]


def split_kernel(received, coef_own, up_1, up_2, down_1, down_2, across):
    kc = lax.axis_index("kc")
    mine = row_coefficients(coef_own)
    for n in range(32):
        up_1[n] = row_block(received, n)
        down_2[n] = row_block(received, n)
        up_2[n] = row_block(received, 32 + n)
        down_1[n] = row_block(received, 32 + n)
    for step, target, at in ((1, up_1, 32), (3, down_1, 32), (2, across, 0)):
        put_pieces(received, (kc + step) % 4, target, at)
        target[at + 4] = mine


def collect_kernel(received, left_1, right_1, far_coef, collected):
    put_pieces(received, lax.axis_index("kc"), collected, 0)
    for n in range(4):
        collected[4 + n] = left_1[32 + n]
        collected[8 + n] = right_1[32 + n]
        collected[12 + n] = far_coef[n]


def spread(row_of, count):
    keep = iota((8, LANES), 1) // PAIRS == iota((8, LANES), 0)
    pieces = []
    for p in range(count):
        for half in range(2):
            pieces.append(jnp.where(keep, jnp.broadcast_to(row_of(p, half), (8, LANES)), 0.0))
    return jnp.concatenate(pieces, axis=0).astype(BF16)


def repeat_matrix():
    same = iota((LANES, LANES), 0) % PAIRS == iota((LANES, LANES), 1) % PAIRS
    return jnp.where(same, 1.0, 0.0).astype(BF16)


def pair_blocks(low_of, high_of, pairs):
    low = iota((PAIRS, LANES), 1) < 64
    for n in range(64):
        first, second = low_of(n), high_of(n)
        pairs[2 * n] = jnp.where(low, first, pltpu.roll(second.astype(F32), 64, 1).astype(BF16))
        pairs[2 * n + 1] = jnp.where(low, pltpu.roll(first.astype(F32), 64, 1).astype(BF16), second)


def turn_points(scalars, first, pairs, turn, picked, turned, v):
    for i in range(64):
        picked[v % 2, i * PAIRS : (i + 1) * PAIRS, :] = pairs[scalars[0, first + 64 * v + i]]
    turned[:, v * 1024 : (v + 1) * 1024] = dot_t(turn, picked[v % 2]).astype(BF16)


def expand_points(turned, cols, result, v):
    for u in range(8 * v, 8 * v + 8):
        at = slice(u * LANES, (u + 1) * LANES)
        result[:, at] = jnp.dot(turned[:, at], cols[u], preferred_element_type=F32).astype(BF16)


def row_copy(result, out, sem, n, step, v):
    row = pl.multiple_of((lax.axis_index("kc") + step) % 4 * 64, 64)
    at = pl.ds(v * 1024, 1024)
    return pltpu.make_async_copy(result.at[pl.ds(n * 64, 64), at], out.at[pl.ds(row, 64), at], sem.at[1 + 4 * n + v])


def diagonal():
    same = iota((LANES, LANES), 0) // PAIRS == iota((LANES, LANES), 1) // PAIRS
    return jnp.where(same, 1.0, 0.0).astype(BF16)


def turn_of(first, second, repeat, diag):
    rows = (first.astype(F32), second.astype(F32))

    def row_of(p, half):
        at = half * POINTS + p % POINTS
        return rows[p // POINTS][at : at + 1]

    return jnp.dot(spread(row_of, 8), repeat, preferred_element_type=F32).astype(BF16) * diag


def turn_kernel(near, received, coef_own, left_1, left_2, turned, pairs, picked, scalars, sem):
    fetch = index_copy(near, scalars, sem)
    fetch.start()
    kc = lax.axis_index("kc")
    turn = turn_of(coef_own[...], left_1[36], repeat_matrix(), diagonal())
    pair_blocks(
        lambda n: row_block(received, n), lambda n: left_1[n] if n < 32 else left_2[n - 32], pairs
    )
    fetch.wait()
    for v in range(4):
        turn_points(scalars, 256 * kc, pairs, turn, picked, turned, v)


def middle_kernel(
    coef_half, coef_other, right_1, far_coef, turned, out, cols, turn_far, pieces, diag, result, sem
):
    kc = lax.axis_index("kc")
    repeat = repeat_matrix()
    diag[...] = diagonal()
    turn_far[...] = turn_of(right_1[36], far_coef[4], repeat, diag[...])
    core = lax.axis_index("kf_2")
    for n, step in enumerate((0, 3, 1, 2)):
        for p in range(8):
            for owner, source in ((core, coef_half), (1 - core, coef_other)):
                piece = source[4 * n + p // 2, p % 2 * 8 : p % 2 * 8 + 8, :].astype(F32)
                pieces[(kc + step) % 4, p, pl.ds(pl.multiple_of(owner * 8, 8), 8), :] = piece

    def build(v):
        for s in range(8):
            p_index, h, par = 2 * v + s // 4, s // 2 % 2, s % 2

            def row_of(p, half):
                r = h * 8 + half * POINTS + p % POINTS
                return pieces[par * 2 + p // POINTS, p_index, r : r + 1, :]

            cols[8 * v + s] = dot_t(repeat, spread(row_of, 8)).astype(BF16) * diag[...]

    for v in range(5):
        if v < 4:
            build(v)
        if v > 0:
            expand_points(turned, cols, result, v - 1)
            for n, step in enumerate((0, 3)):
                row_copy(result, out, sem, n, step, v - 1).start()
    for v in range(4):
        for n, step in enumerate((0, 3)):
            row_copy(result, out, sem, n, step, v).wait()


def last_kernel(near, right_1, right_2, far_1, far_2, cols, turn_far, partial, out, pairs, picked, turned, result, scalars, sem):
    fetch = index_copy(near, scalars, sem)
    fetch.start()
    kc = lax.axis_index("kc")
    pair_blocks(
        lambda n: right_2[n] if n < 32 else right_1[n - 32], lambda n: far_1[n] if n < 32 else far_2[n - 32], pairs
    )
    turn = turn_far[...]
    fetch.wait()
    for v in range(5):
        if v < 4:
            turn_points(scalars, 256 * kc, pairs, turn, picked, turned, v)
        if v > 0:
            expand_points(turned, cols, result, v - 1)
            for n, step in enumerate((1, 2)):
                row_copy(result, out, sem, n, step, v - 1).start()
    for v in range(4):
        for n, step in enumerate((1, 2)):
            row_copy(result, out, sem, n, step, v).wait()


def call(kernel, outs, in_specs, out_specs, scratch, flops, aliases=None):
    return pl.pallas_call(
        kernel,
        out_shape=outs,
        in_specs=in_specs,
        out_specs=out_specs,
        scratch_shapes=scratch,
        input_output_aliases=aliases or {},
        compiler_params=pltpu.CompilerParams(vmem_limit_bytes=8 << 20),
        cost_estimate=pl.CostEstimate(flops=flops, bytes_accessed=flops // 10, transcendentals=0),
    )


def shape(*dims):
    return jax.ShapeDtypeStruct(dims, BF16)


def shift(value, by):
    return lax.ppermute(value, "kc", [(i, (i + by) % 4) for i in range(4)])


def partner(value):
    return lax.ppermute(value, "kf_2", [(0, 1), (1, 0)])


def shards(kernel_coarse, coefficients, nearest):
    other = partner(kernel_coarse)
    rotations = (128, 32, LANES)
    block = (PAIRS, LANES)
    table = jnp.pad(nearest.reshape(1, FINE), ((32, 15), (0, FINE))).astype(F32)
    rows = jnp.pad(coefficients.astype(F32), ((40, 4), (0, 2 * FINE - 2 * LANES)))
    fetched = jnp.pad(kernel_coarse.astype(F32), ((0, 16), (0, 0))) + table + rows
    scalars = [pltpu.SMEM((1, FINE), jnp.int32), pltpu.SemaphoreType.DMA((9,))]
    index = jax.ShapeDtypeStruct((1, FINE), jnp.int32)
    own_copies, near, slots, coef_own = call(
        own_kernel, (shape(*rotations), index, index, shape(8, LANES)), [VMEM], (VMEM,) * 4, [], 1000000
    )(fetched)
    packed = call(
        pack_kernel, shape(PEERS, 40, LANES), [VMEM] * 4, VMEM, [pltpu.VMEM(rotations, BF16)] + scalars, 1000000
    )(slots, own_copies, other, coef_own)
    received = lax.all_to_all(packed, ZY, split_axis=0, concat_axis=0, tiled=True)
    sizes = (37, 32, 37, 32, 5)
    up_1, up_2, down_1, down_2, across = call(
        split_kernel, tuple(shape(n, *block) for n in sizes), [VMEM] * 2, (VMEM,) * 5, [], 100000
    )(received, coef_own)
    left_1 = shift(up_1, 1)
    right_1 = shift(down_1, -1)
    far_coef = shift(across, 2)
    left_2 = shift(up_2, 1)
    right_2 = shift(down_2, -1)
    far_1 = shift(left_1[:PEERS], 1)
    far_2 = shift(right_1[:PEERS], -1)
    coef_half = call(collect_kernel, shape(16, *block), [VMEM] * 4, VMEM, [], 100000)(received, left_1, right_1, far_coef)
    coef_other = partner(coef_half)
    pairs = pltpu.VMEM((128, *block), BF16)
    picked = pltpu.VMEM((2, 1024, LANES), BF16)
    turned = pltpu.VMEM((LANES, 4096), BF16)
    rows_turned = call(
        turn_kernel, shape(LANES, 4096), [VMEM] * 5, VMEM, [pairs, picked] + scalars, 2000000
    )(near, received, coef_own, left_1, left_2)
    partial, cols, turn_far = call(
        middle_kernel,
        (shape(256, 4096), shape(32, LANES, LANES), shape(LANES, LANES)),
        [VMEM] * 5,
        (ANY, VMEM, VMEM),
        [pltpu.VMEM((4, 8, *block), F32), pltpu.VMEM((LANES, LANES), BF16), turned] + scalars[1:],
        8000000,
    )(coef_half, coef_other, right_1, far_coef, rows_turned)
    return call(
        last_kernel,
        shape(256, 4096),
        [VMEM] * 7 + [ANY],
        ANY,
        [pairs, picked, turned, turned] + scalars,
        3000000,
        {7: 0},
    )(near, right_1, right_2, far_1, far_2, cols, turn_far, partial)


def solution(mesh):
    split = Mesh(mesh.devices.reshape(8, 4, 2, mesh.shape["kc"]), KF_KC)
    return jax.shard_map(
        shards,
        mesh=split,
        in_specs=(P(KF, None), P(KF_KC, None), P()),
        out_specs=P(KF, "kc"),
        check_vma=False,
    )
```

profile of v0, /device:TPU:1, one launch (start us, length us, event | category | flops | bytes accessed | tf_op | source)
XLA Modules:
  0.0 53.1 jit_solution(16334394556701800244)
XLA Ops:
  0.0 3.2 %collective-permute-start = (bf16[32,2048]{1,0:T(8,128)(2,1)}, bf16[32,2048]{1,0:T(8,128)(2,1)S(1)}, u32[]{:S(2)}, u32[]{:S(2)}) collective-permute-start(bf16[32,2048]{1,0:T(8,128)(2,1)} %param.3), channel_id=1, source_target_pairs={{0,4},{4,0},{1,5},{5,1},{2,6},{6,2},{3,7},{7,3},{8,12},{12,8},{9,1... | collective-permute-start | bytes 393224 | tf_op jit(solution)/shard_map/ppermute | solution.py:266
  3.2 1.0 %convert_add_fusion.fetched = f32[48,2048]{1,0:T(8,128)S(1)} fusion(s32[1,1024]{1,0:T(1,128)} %bitcast.1, bf16[4,256]{1,0:T(4,128)(2,1)} %param.4, bf16[32,2048]{1,0:T(8,128)(2,1)} %param.3), kind=kLoop, calls=%fused_computation | loop fusion | flops 491520 | bytes 530432 | tf_op jit(solution)/shard_map/add | solution.py:275
  4.2 0.3 shard_map.37
  4.5 1.4 %shard_map.38 = bf16[32,40,128]{2,1,0:T(8,128)(2,1)S(1)} custom-call(s32[1,1024]{1,0:T(1,128)S(1)} %get-tuple-element.18.slots, bf16[128,32,128]{2,1,0:T(8,128)(2,1)S(1)} %get-tuple-element.19.own_copies, bf16[32,2048]{1,0:T(8,128)(2,1)S(1)} %collective-permute-done.other, bf16[8,128]{1,0:T(8,128)(2,1)S(1)} %get-tuple-element.20.coef.coef_own), custom_call_target="tpu_custom_call" | custom-call | flops 1000000 | bytes 100000 | tf_op jit(solution)/shard_map/pallas_call | solution.py:281
  5.9 22.2 %all_to_all.5.received = bf16[32,40,128]{2,1,0:T(8,128)(2,1)S(1)} all-to-all(bf16[32,40,128]{2,1,0:T(8,128)(2,1)S(1)} %shard_map.38), channel_id=1, replica_groups=mesh['kf_0'=8,'kf_1'=4,'kf_2'=2,'kc'=4] {'kf_0','kf_1'}, dimensions={0} | all-to-all | bytes 655360 | tf_op jit(solution)/shard_map/all_to_all | solution.py:284
  28.0 0.1 shard_map.39
  28.1 2.6 %collective-permute-start.1 = (bf16[37,16,128]{2,1,0:T(8,128)(2,1)S(1)}, bf16[37,16,128]{2,1,0:T(8,128)(2,1)S(1)}, u32[]{:S(2)}, u32[]{:S(2)}) collective-permute-start(bf16[37,16,128]{2,1,0:T(8,128)(2,1)S(1)} %get-tuple-element.21), channel_id=1, source_target_pairs={{0,3},{1,0},{2,1},{3,2},{4,7},{5,4},{6,5},{7,6},{8,11},{9,8},{10,9... | collective-permute-start | bytes 454664 | tf_op jit(solution)/shard_map/ppermute | solution.py:262
  30.7 0.0 collective-permute-start.3
  30.7 0.2 collective-permute-start.8
  30.9 2.5 %collective-permute-start.2 = (bf16[32,16,128]{2,1,0:T(8,128)(2,1)S(1)}, bf16[32,16,128]{2,1,0:T(8,128)(2,1)S(1)}, u32[]{:S(2)}, u32[]{:S(2)}) collective-permute-start(bf16[32,16,128]{2,1,0:T(8,128)(2,1)S(1)} %get-tuple-element.22), channel_id=1, source_target_pairs={{0,3},{1,0},{2,1},{3,2},{4,7},{5,4},{6,5},{7,6},{8,11},{9,8},{10,9... | collective-permute-start | bytes 393224 | tf_op jit(solution)/shard_map/ppermute | solution.py:262
  33.4 0.0 collective-permute-done.1.right_1
  33.4 2.6 %collective-permute-start.5 = (bf16[32,16,128]{2,1,0:T(8,128)(2,1)S(1)}, bf16[32,16,128]{2,1,0:T(8,128)(2,1)S(1)}, u32[]{:S(2)}, u32[]{:S(2)}) collective-permute-start(bf16[32,16,128]{2,1,0:T(8,128)(2,1)S(1)} %slice.9), channel_id=1, source_target_pairs={{0,3},{1,0},{2,1},{3,2},{4,7},{5,4},{6,5},{7,6},{8,11},{9,8},{10,9... | collective-permute-start | bytes 393224 | tf_op jit(solution)/shard_map/ppermute | solution.py:262
  36.0 0.0 collective-permute-done.3.left_1
  36.0 0.1 collective-permute-start.4
  36.1 1.2 %collective-permute-start.6 = (bf16[5,16,128]{2,1,0:T(8,128)(2,1)S(1)}, bf16[5,16,128]{2,1,0:T(8,128)(2,1)S(1)}, u32[]{:S(2)}, u32[]{:S(2)}) collective-permute-start(bf16[5,16,128]{2,1,0:T(8,128)(2,1)S(1)} %get-tuple-element.24), channel_id=1, source_target_pairs={{0,2},{1,3},{2,0},{3,1},{4,6},{5,7},{6,4},{7,5},{8,10},{9,11},{10,... | collective-permute-start | bytes 61448 | tf_op jit(solution)/shard_map/ppermute | solution.py:262
  37.3 4.1 %collective-permute-done.6.far_coef = bf16[5,16,128]{2,1,0:T(8,128)(2,1)S(1)} collective-permute-done((bf16[5,16,128]{2,1,0:T(8,128)(2,1)S(1)}, bf16[5,16,128]{2,1,0:T(8,128)(2,1)S(1)}, u32[]{:S(2)}, u32[]{:S(2)}) %collective-permute-start.6) | collective-permute-done | bytes 20512 | tf_op jit(solution)/shard_map/ppermute | solution.py:262
  41.5 5.6 %collective-permute-start.7 = (bf16[16,16,128]{2,1,0:T(8,128)(2,1)S(1)}, bf16[16,16,128]{2,1,0:T(8,128)(2,1)S(1)}, u32[]{:S(2)}, u32[]{:S(2)}) collective-permute-start(bf16[16,16,128]{2,1,0:T(8,128)(2,1)S(1)} %shard_map.40.coef_half), channel_id=1, source_target_pairs={{0,4},{4,0},{1,5},{5,1},{2,6},{6,2},{3,7},{7,3},{8,12},{12,8},{9,1... | collective-permute-start | bytes 196616 | tf_op jit(solution)/shard_map/ppermute | solution.py:266
  47.0 0.0 collective-permute-done.8.left_2
  47.0 1.4 %shard_map.41.turned = bf16[128,4096]{1,0:T(8,128)(2,1)S(1)} custom-call(s32[1,1024]{1,0:T(1,128)S(1)} %get-tuple-element.17.near, bf16[32,40,128]{2,1,0:T(8,128)(2,1)S(1)} %all_to_all.5.received, bf16[8,128]{1,0:T(8,128)(2,1)S(1)} %get-tuple-element.20.coef.coef_own, bf16[37,16,128]{2,1,0:T(8,128)(2,1)S(1)} %collective-permute-done.3.left_1, ...), custom_call_target="tpu_custom_call" | custom-call | flops 2000000 | bytes 200000 | tf_op jit(solution)/shard_map/pallas_call | solution.py:301
  48.4 0.0 collective-permute-done.7.coef_other
  48.4 2.1 %shard_map.42 = (bf16[256,4096]{1,0:T(8,128)(2,1)}, bf16[32,128,128]{2,1,0:T(8,128)(2,1)S(1)}, bf16[128,128]{1,0:T(8,128)(2,1)S(1)}) custom-call(bf16[16,16,128]{2,1,0:T(8,128)(2,1)S(1)} %shard_map.40.coef_half, bf16[16,16,128]{2,1,0:T(8,128)(2,1)S(1)} %collective-permute-done.7.coef_other, bf16[37,16,128]{2,1,0:T(8,128)(2,1)S(1)} %collective-permute-done.1.right_1, ...), custom_call_target="tpu_custom_call" | custom-call | flops 8000000 | bytes 800000 | tf_op jit(solution)/shard_map/pallas_call | solution.py:304
  50.5 0.0 collective-permute-done.2.right_2
  50.5 0.0 collective-permute-done.4.far_1
  50.5 2.5 %shard_map.43 = bf16[256,4096]{1,0:T(8,128)(2,1)} custom-call(s32[1,1024]{1,0:T(1,128)S(1)} %get-tuple-element.17.near, bf16[37,16,128]{2,1,0:T(8,128)(2,1)S(1)} %collective-permute-done.1.right_1, bf16[32,16,128]{2,1,0:T(8,128)(2,1)S(1)} %collective-permute-done.2.right_2, ...), custom_call_target="tpu_custom_call", output_to_operand_aliasing={{}: (7, {})} | custom-call | flops 3000000 | bytes 300000 | tf_op jit(solution)/shard_map/pallas_call | solution.py:312
  (5 shorter events, 0.0 us)
Async XLA Ops:
  0.0 4.5 %collective-permute-start = (bf16[32,2048]{1,0:T(8,128)(2,1)}, bf16[32,2048]{1,0:T(8,128)(2,1)S(1)}, u32[]{:S(2)}, u32[]{:S(2)}) collective-permute-start(bf16[32,2048]{1,0:T(8,128)(2,1)} %param.3), channel_id=1, source_target_pairs={{0,4},{4,0},{1,5},{5,1},{2,6},{6,2},{3,7},{7,3},{8,12},{12,8},{9,1... | collective-permute-start | bytes 393224 | tf_op jit(solution)/shard_map/ppermute | solution.py:266
  28.1 5.3 %collective-permute-start.1 = (bf16[37,16,128]{2,1,0:T(8,128)(2,1)S(1)}, bf16[37,16,128]{2,1,0:T(8,128)(2,1)S(1)}, u32[]{:S(2)}, u32[]{:S(2)}) collective-permute-start(bf16[37,16,128]{2,1,0:T(8,128)(2,1)S(1)} %get-tuple-element.21), channel_id=1, source_target_pairs={{0,3},{1,0},{2,1},{3,2},{4,7},{5,4},{6,5},{7,6},{8,11},{9,8},{10,9... | collective-permute-start | bytes 454664 | tf_op jit(solution)/shard_map/ppermute | solution.py:262
  30.7 5.3 %collective-permute-start.3 = (bf16[37,16,128]{2,1,0:T(8,128)(2,1)S(1)}, bf16[37,16,128]{2,1,0:T(8,128)(2,1)S(1)}, u32[]{:S(2)}, u32[]{:S(2)}) collective-permute-start(bf16[37,16,128]{2,1,0:T(8,128)(2,1)S(1)} %get-tuple-element.23), channel_id=1, source_target_pairs={{0,1},{1,2},{2,3},{3,0},{4,5},{5,6},{6,7},{7,4},{8,9},{9,10},{10,1... | collective-permute-start | bytes 454664 | tf_op jit(solution)/shard_map/ppermute | solution.py:262
  30.7 16.4 %collective-permute-start.8 = (bf16[32,16,128]{2,1,0:T(8,128)(2,1)S(1)}, bf16[32,16,128]{2,1,0:T(8,128)(2,1)S(1)}, u32[]{:S(2)}, u32[]{:S(2)}) collective-permute-start(bf16[32,16,128]{2,1,0:T(8,128)(2,1)S(1)} %get-tuple-element.25), channel_id=1, source_target_pairs={{0,1},{1,2},{2,3},{3,0},{4,5},{5,6},{6,7},{7,4},{8,9},{9,10},{10,1... | collective-permute-start | bytes 393224 | tf_op jit(solution)/shard_map/ppermute | solution.py:262
  30.9 19.6 %collective-permute-start.2 = (bf16[32,16,128]{2,1,0:T(8,128)(2,1)S(1)}, bf16[32,16,128]{2,1,0:T(8,128)(2,1)S(1)}, u32[]{:S(2)}, u32[]{:S(2)}) collective-permute-start(bf16[32,16,128]{2,1,0:T(8,128)(2,1)S(1)} %get-tuple-element.22), channel_id=1, source_target_pairs={{0,3},{1,0},{2,1},{3,2},{4,7},{5,4},{6,5},{7,6},{8,11},{9,8},{10,9... | collective-permute-start | bytes 393224 | tf_op jit(solution)/shard_map/ppermute | solution.py:262
  33.4 17.1 %collective-permute-start.5 = (bf16[32,16,128]{2,1,0:T(8,128)(2,1)S(1)}, bf16[32,16,128]{2,1,0:T(8,128)(2,1)S(1)}, u32[]{:S(2)}, u32[]{:S(2)}) collective-permute-start(bf16[32,16,128]{2,1,0:T(8,128)(2,1)S(1)} %slice.9), channel_id=1, source_target_pairs={{0,3},{1,0},{2,1},{3,2},{4,7},{5,4},{6,5},{7,6},{8,11},{9,8},{10,9... | collective-permute-start | bytes 393224 | tf_op jit(solution)/shard_map/ppermute | solution.py:262
  36.0 14.5 %collective-permute-start.4 = (bf16[32,16,128]{2,1,0:T(8,128)(2,1)S(1)}, bf16[32,16,128]{2,1,0:T(8,128)(2,1)S(1)}, u32[]{:S(2)}, u32[]{:S(2)}) collective-permute-start(bf16[32,16,128]{2,1,0:T(8,128)(2,1)S(1)} %slice.8), channel_id=1, source_target_pairs={{0,1},{1,2},{2,3},{3,0},{4,5},{5,6},{6,7},{7,4},{8,9},{9,10},{10,1... | collective-permute-start | bytes 393224 | tf_op jit(solution)/shard_map/ppermute | solution.py:262
  36.1 5.3 %collective-permute-start.6 = (bf16[5,16,128]{2,1,0:T(8,128)(2,1)S(1)}, bf16[5,16,128]{2,1,0:T(8,128)(2,1)S(1)}, u32[]{:S(2)}, u32[]{:S(2)}) collective-permute-start(bf16[5,16,128]{2,1,0:T(8,128)(2,1)S(1)} %get-tuple-element.24), channel_id=1, source_target_pairs={{0,2},{1,3},{2,0},{3,1},{4,6},{5,7},{6,4},{7,5},{8,10},{9,11},{10,... | collective-permute-start | bytes 61448 | tf_op jit(solution)/shard_map/ppermute | solution.py:262
  41.5 6.9 %collective-permute-start.7 = (bf16[16,16,128]{2,1,0:T(8,128)(2,1)S(1)}, bf16[16,16,128]{2,1,0:T(8,128)(2,1)S(1)}, u32[]{:S(2)}, u32[]{:S(2)}) collective-permute-start(bf16[16,16,128]{2,1,0:T(8,128)(2,1)S(1)} %shard_map.40.coef_half), channel_id=1, source_target_pairs={{0,4},{4,0},{1,5},{5,1},{2,6},{6,2},{3,7},{7,3},{8,12},{12,8},{9,1... | collective-permute-start | bytes 196616 | tf_op jit(solution)/shard_map/ppermute | solution.py:266
where the time goes:
time: 53.2 us; the launch traced here: 53.1 us
  blocking collectives  22.2 us (42%)
  starting transfers between devices  17.9 us (34%)
  Pallas kernels  7.72 us (15%)
  waiting for transfers between devices  4.17 us (8%)
  other arithmetic  0.96 us (2%)
    all_to_all x1, blocking collectives, shards(): lax.all_to_all(packed, ZY, split_axis=0, concat_axis=0, tiled=True)  22.2 us
    ppermute x7, starting transfers between devices, shift(): return lax.ppermute(value, 'kc', [(i, (i + by) % 4) for i in range(4)])  9.15 us
    ppermute x2, starting transfers between devices, partner(): return lax.ppermute(value, 'kf_2', [(0, 1), (1, 0)])  8.77 us
    ppermute x7, waiting for transfers between devices, shift(): return lax.ppermute(value, 'kc', [(i, (i + by) % 4) for i in range(4)])  4.16 us
    pallas_call x1, Pallas kernels, shards(): call(last_kernel, shape(256, 4096), [VMEM] * 7 + [ANY], ANY, [pairs, pick...  2.52 us
    pallas_call x1, Pallas kernels, shards(): call(middle_kernel, (shape(256, 4096), shape(32, LANES, LANES), shape(LAN...  2.07 us
    pallas_call x1, Pallas kernels, shards(): call(pack_kernel, shape(PEERS, 40, LANES), [VMEM] * 4, VMEM, [pltpu.VMEM(...  1.38 us
    pallas_call x1, Pallas kernels, shards(): call(turn_kernel, shape(LANES, 4096), [VMEM] * 5, VMEM, [pairs, picked] +...  1.36 us
  transfers between devices with their start and end apart: 9, of which 1 were waited for; matrix products, arithmetic and copies ran while one was open for 2% of the time, Pallas kernels for 7%

commit v1 on v0

--- a/solution.py
+++ b/solution.py
@@ -14,6 +14,7 @@
 PAIRS = 16
 POINTS = 4
 PEERS = 32
+RISING = 44
 FINE = 1024
 BF16 = jnp.bfloat16
 F32 = jnp.float32
@@ -42,23 +43,20 @@
     return jnp.concatenate([coef[:, :LANES], coef[:, LANES:]], axis=0)
 
 
-def own_kernel(fetched, copies, near, slots, coef):
-    c = fetched[32:33, :FINE].astype(jnp.int32)
-    near[...] = c
-    slots[...] = ((iota((1, FINE), 1) % POINTS - c) & 7) * 16 + (c >> 3)
-    coef[...] = halves_stacked(fetched[40:44, : 2 * LANES]).astype(BF16)
-    turn_rows(fetched, copies)
-
-
 def index_copy(near, scalars, sem):
     return pltpu.make_async_copy(near, scalars, sem.at[0])
 
 
-def pack_kernel(slots, own_copies, other, coef, out, other_copies, scalars, sem):
+def pack_kernel(fetched, other, out, near, coef, own_copies, other_copies, slots, scalars, sem):
+    c = fetched[32:33, :FINE].astype(jnp.int32)
+    slots[...] = ((iota((1, FINE), 1) % POINTS - c) & 7) * 16 + (c >> 3)
     fetch = index_copy(slots, scalars, sem)
     fetch.start()
+    near[...] = c
+    coef[...] = halves_stacked(fetched[40:44, : 2 * LANES]).astype(BF16)
     kc = lax.axis_index("kc")
     core = lax.axis_index("kf_2")
+    turn_rows(fetched, own_copies)
     turn_rows(other, other_copies)
     copies = (own_copies, other_copies)
     fetch.wait()
@@ -98,12 +96,15 @@
 def split_kernel(received, coef_own, up_1, up_2, down_1, down_2, across):
     kc = lax.axis_index("kc")
     mine = row_coefficients(coef_own)
-    for n in range(32):
-        up_1[n] = row_block(received, n)
-        down_2[n] = row_block(received, n)
-        up_2[n] = row_block(received, 32 + n)
-        down_1[n] = row_block(received, 32 + n)
-    for step, target, at in ((1, up_1, 32), (3, down_1, 32), (2, across, 0)):
+    for n in range(64):
+        block = row_block(received, n)
+        if n < RISING:
+            up_1[n] = block
+            down_2[n] = block
+        else:
+            up_2[n - RISING] = block
+            down_1[n - RISING] = block
+    for step, target, at in ((1, up_1, RISING), (3, down_1, 64 - RISING), (2, across, 0)):
         put_pieces(received, (kc + step) % 4, target, at)
         target[at + 4] = mine
 
@@ -111,8 +112,8 @@
 def collect_kernel(received, left_1, right_1, far_coef, collected):
     put_pieces(received, lax.axis_index("kc"), collected, 0)
     for n in range(4):
-        collected[4 + n] = left_1[32 + n]
-        collected[8 + n] = right_1[32 + n]
+        collected[4 + n] = left_1[RISING + n]
+        collected[8 + n] = right_1[64 - RISING + n]
         collected[12 + n] = far_coef[n]
 
 
@@ -175,9 +176,9 @@
     fetch = index_copy(near, scalars, sem)
     fetch.start()
     kc = lax.axis_index("kc")
-    turn = turn_of(coef_own[...], left_1[36], repeat_matrix(), diagonal())
+    turn = turn_of(coef_own[...], left_1[RISING + 4], repeat_matrix(), diagonal())
     pair_blocks(
-        lambda n: row_block(received, n), lambda n: left_1[n] if n < 32 else left_2[n - 32], pairs
+        lambda n: row_block(received, n), lambda n: left_1[n] if n < RISING else left_2[n - RISING], pairs
     )
     fetch.wait()
     for v in range(4):
@@ -190,7 +191,7 @@
     kc = lax.axis_index("kc")
     repeat = repeat_matrix()
     diag[...] = diagonal()
-    turn_far[...] = turn_of(right_1[36], far_coef[4], repeat, diag[...])
+    turn_far[...] = turn_of(right_1[68 - RISING], far_coef[4], repeat, diag[...])
     core = lax.axis_index("kf_2")
     for n, step in enumerate((0, 3, 1, 2)):
         for p in range(8):
@@ -225,7 +226,9 @@
     fetch.start()
     kc = lax.axis_index("kc")
     pair_blocks(
-        lambda n: right_2[n] if n < 32 else right_1[n - 32], lambda n: far_1[n] if n < 32 else far_2[n - 32], pairs
+        lambda n: right_2[n] if n < RISING else right_1[n - RISING],
+        lambda n: far_1[n] if n < RISING else far_2[n - RISING],
+        pairs,
     )
     turn = turn_far[...]
     fetch.wait()
@@ -274,15 +277,17 @@
     rows = jnp.pad(coefficients.astype(F32), ((40, 4), (0, 2 * FINE - 2 * LANES)))
     fetched = jnp.pad(kernel_coarse.astype(F32), ((0, 16), (0, 0))) + table + rows
     scalars = [pltpu.SMEM((1, FINE), jnp.int32), pltpu.SemaphoreType.DMA((9,))]
-    index = jax.ShapeDtypeStruct((1, FINE), jnp.int32)
-    own_copies, near, slots, coef_own = call(
-        own_kernel, (shape(*rotations), index, index, shape(8, LANES)), [VMEM], (VMEM,) * 4, [], 1000000
-    )(fetched)
-    packed = call(
-        pack_kernel, shape(PEERS, 40, LANES), [VMEM] * 4, VMEM, [pltpu.VMEM(rotations, BF16)] + scalars, 1000000
-    )(slots, own_copies, other, coef_own)
+    copies = pltpu.VMEM(rotations, BF16)
+    packed, near, coef_own = call(
+        pack_kernel,
+        (shape(PEERS, 40, LANES), jax.ShapeDtypeStruct((1, FINE), jnp.int32), shape(8, LANES)),
+        [VMEM] * 2,
+        (VMEM,) * 3,
+        [copies, copies, pltpu.VMEM((1, FINE), jnp.int32)] + scalars,
+        1000000,
+    )(fetched, other)
     received = lax.all_to_all(packed, ZY, split_axis=0, concat_axis=0, tiled=True)
-    sizes = (37, 32, 37, 32, 5)
+    sizes = (RISING + 5, 64 - RISING, 69 - RISING, RISING, 5)
     up_1, up_2, down_1, down_2, across = call(
         split_kernel, tuple(shape(n, *block) for n in sizes), [VMEM] * 2, (VMEM,) * 5, [], 100000
     )(received, coef_own)
@@ -291,8 +296,8 @@
     far_coef = shift(across, 2)
     left_2 = shift(up_2, 1)
     right_2 = shift(down_2, -1)
-    far_1 = shift(left_1[:PEERS], 1)
-    far_2 = shift(right_1[:PEERS], -1)
+    far_1 = shift(left_1[:RISING], 1)
+    far_2 = shift(right_1[: 64 - RISING], -1)
     coef_half = call(collect_kernel, shape(16, *block), [VMEM] * 4, VMEM, [], 100000)(received, left_1, right_1, far_coef)
     coef_other = partner(coef_half)
     pairs = pltpu.VMEM((128, *block), BF16)

time: 53.2 us -> 50.9 us (0.957)
  waiting for transfers between devices: 4.17 us -> 2.72 us
  starting transfers between devices: 17.9 us -> 17.2 us
    ppermute x7, waiting for transfers between devices: 4.16 us -> 2.49 us  [shift(): return lax.ppermute(value, 'kc', [(i, (i + by) % 4) for i in range(4)])]
    ppermute x2, starting transfers between devices: 8.77 us -> 7.95 us  [partner(): return lax.ppermute(value, 'kf_2', [(0, 1), (1, 0)])]
    pallas_call x2 -> x1, Pallas kernels: 1.68 us -> 1.6 us  [shards(): call(pack_kernel, (shape(PEERS, 40, LANES), jax.ShapeDtypeStruct((1, FINE...]
  transfers between devices with their start and end apart: 9 -> 9, of which waited for: 1 -> 3; matrix products, arithmetic and copies ran while one was open for 2% -> 2% of each run, Pallas kernels for 7% -> 7%
where the time goes in v1:
time: 50.9 us; the launch traced here: 50.7 us
  blocking collectives  22.1 us (43%)
  starting transfers between devices  17.2 us (34%)
  Pallas kernels  7.63 us (15%)
  waiting for transfers between devices  2.72 us (5%)
  other arithmetic  0.96 us (2%)
    all_to_all x1, blocking collectives, shards(): lax.all_to_all(packed, ZY, split_axis=0, concat_axis=0, tiled=True)  22.1 us
    ppermute x7, starting transfers between devices, shift(): return lax.ppermute(value, 'kc', [(i, (i + by) % 4) for i in range(4)])  9.3 us
    ppermute x2, starting transfers between devices, partner(): return lax.ppermute(value, 'kf_2', [(0, 1), (1, 0)])  7.95 us
    pallas_call x1, Pallas kernels, shards(): call(last_kernel, shape(256, 4096), [VMEM] * 7 + [ANY], ANY, [pairs, pick...  2.51 us
    ppermute x7, waiting for transfers between devices, shift(): return lax.ppermute(value, 'kc', [(i, (i + by) % 4) for i in range(4)])  2.49 us
    pallas_call x1, Pallas kernels, shards(): call(middle_kernel, (shape(256, 4096), shape(32, LANES, LANES), shape(LAN...  2.08 us
    pallas_call x1, Pallas kernels, shards(): call(pack_kernel, (shape(PEERS, 40, LANES), jax.ShapeDtypeStruct((1, FINE...  1.6 us
    pallas_call x1, Pallas kernels, shards(): call(turn_kernel, shape(LANES, 4096), [VMEM] * 5, VMEM, [pairs, picked] +...  1.36 us
  transfers between devices with their start and end apart: 9, of which 3 were waited for; matrix products, arithmetic and copies ran while one was open for 2% of the time, Pallas kernels for 7%

profile of v1, /device:TPU:1, one launch (start us, length us, event | category | flops | bytes accessed | tf_op | source)
XLA Modules:
  0.0 50.7 jit_solution(13322403353264741459)
XLA Ops:
  0.0 3.2 %collective-permute-start = (bf16[32,2048]{1,0:T(8,128)(2,1)}, bf16[32,2048]{1,0:T(8,128)(2,1)S(1)}, u32[]{:S(2)}, u32[]{:S(2)}) collective-permute-start(bf16[32,2048]{1,0:T(8,128)(2,1)} %param.3), channel_id=1, source_target_pairs={{0,4},{4,0},{1,5},{5,1},{2,6},{6,2},{3,7},{7,3},{8,12},{12,8},{9,1... | collective-permute-start | bytes 393224 | tf_op jit(solution)/shard_map/ppermute | solution.py:269
  3.2 1.0 %convert_add_fusion.fetched = f32[48,2048]{1,0:T(8,128)S(1)} fusion(s32[1,1024]{1,0:T(1,128)} %bitcast.1, bf16[4,256]{1,0:T(4,128)(2,1)} %param.4, bf16[32,2048]{1,0:T(8,128)(2,1)} %param.3), kind=kLoop, calls=%fused_computation | loop fusion | flops 491520 | bytes 530432 | tf_op jit(solution)/shard_map/add | solution.py:278
  4.2 0.2 collective-permute-done.other
  4.4 1.6 %shard_map.37 = (bf16[32,40,128]{2,1,0:T(8,128)(2,1)S(1)}, s32[1,1024]{1,0:T(1,128)S(1)}, bf16[8,128]{1,0:T(8,128)(2,1)S(1)}) custom-call(f32[48,2048]{1,0:T(8,128)S(1)} %convert_add_fusion.fetched, bf16[32,2048]{1,0:T(8,128)(2,1)S(1)} %collective-permute-done.other), custom_call_target="tpu_custom_call" | custom-call | flops 1000000 | bytes 100000 | tf_op jit(solution)/shard_map/pallas_call | solution.py:281
  6.0 22.1 %all_to_all.5.received = bf16[32,40,128]{2,1,0:T(8,128)(2,1)S(1)} all-to-all(bf16[32,40,128]{2,1,0:T(8,128)(2,1)S(1)} %get-tuple-element.17), channel_id=1, replica_groups=mesh['kf_0'=8,'kf_1'=4,'kf_2'=2,'kc'=4] {'kf_0','kf_1'}, dimensions={0} | all-to-all | bytes 655360 | tf_op jit(solution)/shard_map/all_to_all | solution.py:289
  28.1 0.1 shard_map.38
  28.2 1.3 %collective-permute-start.3 = (bf16[49,16,128]{2,1,0:T(8,128)(2,1)S(1)}, bf16[49,16,128]{2,1,0:T(8,128)(2,1)S(1)}, u32[]{:S(2)}, u32[]{:S(2)}) collective-permute-start(bf16[49,16,128]{2,1,0:T(8,128)(2,1)S(1)} %get-tuple-element.21), channel_id=1, source_target_pairs={{0,1},{1,2},{2,3},{3,0},{4,5},{5,6},{6,7},{7,4},{8,9},{9,10},{10,1... | collective-permute-start | bytes 602120 | tf_op jit(solution)/shard_map/ppermute | solution.py:265
  29.5 1.5 %collective-permute-start.1 = (bf16[25,16,128]{2,1,0:T(8,128)(2,1)S(1)}, bf16[25,16,128]{2,1,0:T(8,128)(2,1)S(1)}, u32[]{:S(2)}, u32[]{:S(2)}) collective-permute-start(bf16[25,16,128]{2,1,0:T(8,128)(2,1)S(1)} %get-tuple-element.19), channel_id=1, source_target_pairs={{0,3},{1,0},{2,1},{3,2},{4,7},{5,4},{6,5},{7,6},{8,11},{9,8},{10,9... | collective-permute-start | bytes 307208 | tf_op jit(solution)/shard_map/ppermute | solution.py:265
  30.9 1.3 %collective-permute-start.2 = (bf16[44,16,128]{2,1,0:T(8,128)(2,1)S(1)}, bf16[44,16,128]{2,1,0:T(8,128)(2,1)S(1)}, u32[]{:S(2)}, u32[]{:S(2)}) collective-permute-start(bf16[44,16,128]{2,1,0:T(8,128)(2,1)S(1)} %get-tuple-element.20), channel_id=1, source_target_pairs={{0,3},{1,0},{2,1},{3,2},{4,7},{5,4},{6,5},{7,6},{8,11},{9,8},{10,9... | collective-permute-start | bytes 540680 | tf_op jit(solution)/shard_map/ppermute | solution.py:265
  32.2 1.8 %collective-permute-done.3.left_1 = bf16[49,16,128]{2,1,0:T(8,128)(2,1)S(1)} collective-permute-done((bf16[49,16,128]{2,1,0:T(8,128)(2,1)S(1)}, bf16[49,16,128]{2,1,0:T(8,128)(2,1)S(1)}, u32[]{:S(2)}, u32[]{:S(2)}) %collective-permute-start.3) | collective-permute-done | bytes 200736 | tf_op jit(solution)/shard_map/ppermute | solution.py:265
  34.0 0.1 collective-permute-start.4
  34.1 2.4 %collective-permute-start.6 = (bf16[5,16,128]{2,1,0:T(8,128)(2,1)S(1)}, bf16[5,16,128]{2,1,0:T(8,128)(2,1)S(1)}, u32[]{:S(2)}, u32[]{:S(2)}) collective-permute-start(bf16[5,16,128]{2,1,0:T(8,128)(2,1)S(1)} %get-tuple-element.22), channel_id=1, source_target_pairs={{0,2},{1,3},{2,0},{3,1},{4,6},{5,7},{6,4},{7,5},{8,10},{9,11},{10,... | collective-permute-start | bytes 61448 | tf_op jit(solution)/shard_map/ppermute | solution.py:265
  36.6 0.8 %collective-permute-start.8 = (bf16[20,16,128]{2,1,0:T(8,128)(2,1)S(1)}, bf16[20,16,128]{2,1,0:T(8,128)(2,1)S(1)}, u32[]{:S(2)}, u32[]{:S(2)}) collective-permute-start(bf16[20,16,128]{2,1,0:T(8,128)(2,1)S(1)} %get-tuple-element.23), channel_id=1, source_target_pairs={{0,1},{1,2},{2,3},{3,0},{4,5},{5,6},{6,7},{7,4},{8,9},{9,10},{10,1... | collective-permute-start | bytes 245768 | tf_op jit(solution)/shard_map/ppermute | solution.py:265
  37.4 0.0 collective-permute-done.1.right_1
  37.4 2.0 %collective-permute-start.5 = (bf16[20,16,128]{2,1,0:T(8,128)(2,1)S(1)}, bf16[20,16,128]{2,1,0:T(8,128)(2,1)S(1)}, u32[]{:S(2)}, u32[]{:S(2)}) collective-permute-start(bf16[20,16,128]{2,1,0:T(8,128)(2,1)S(1)} %slice.9), channel_id=1, source_target_pairs={{0,3},{1,0},{2,1},{3,2},{4,7},{5,4},{6,5},{7,6},{8,11},{9,8},{10,9... | collective-permute-start | bytes 245768 | tf_op jit(solution)/shard_map/ppermute | solution.py:265
  39.3 0.6 %collective-permute-done.6.far_coef = bf16[5,16,128]{2,1,0:T(8,128)(2,1)S(1)} collective-permute-done((bf16[5,16,128]{2,1,0:T(8,128)(2,1)S(1)}, bf16[5,16,128]{2,1,0:T(8,128)(2,1)S(1)}, u32[]{:S(2)}, u32[]{:S(2)}) %collective-permute-start.6) | collective-permute-done | bytes 20512 | tf_op jit(solution)/shard_map/ppermute | solution.py:265
  40.0 4.7 %collective-permute-start.7 = (bf16[16,16,128]{2,1,0:T(8,128)(2,1)S(1)}, bf16[16,16,128]{2,1,0:T(8,128)(2,1)S(1)}, u32[]{:S(2)}, u32[]{:S(2)}) collective-permute-start(bf16[16,16,128]{2,1,0:T(8,128)(2,1)S(1)} %shard_map.39.coef_half), channel_id=1, source_target_pairs={{0,4},{4,0},{1,5},{5,1},{2,6},{6,2},{3,7},{7,3},{8,12},{12,8},{9,1... | collective-permute-start | bytes 196616 | tf_op jit(solution)/shard_map/ppermute | solution.py:269
  44.7 0.0 collective-permute-done.8.left_2
  44.7 1.4 %shard_map.40.turned = bf16[128,4096]{1,0:T(8,128)(2,1)S(1)} custom-call(s32[1,1024]{1,0:T(1,128)S(1)} %get-tuple-element.16.near, bf16[32,40,128]{2,1,0:T(8,128)(2,1)S(1)} %all_to_all.5.received, bf16[8,128]{1,0:T(8,128)(2,1)S(1)} %get-tuple-element.18.coef_own, bf16[49,16,128]{2,1,0:T(8,128)(2,1)S(1)} %collective-permute-done.3.left_1, ...), custom_call_target="tpu_custom_call" | custom-call | flops 2000000 | bytes 200000 | tf_op jit(solution)/shard_map/pallas_call | solution.py:306
  46.1 0.0 collective-permute-done.7.coef_other
  46.1 2.1 %shard_map.41 = (bf16[256,4096]{1,0:T(8,128)(2,1)}, bf16[32,128,128]{2,1,0:T(8,128)(2,1)S(1)}, bf16[128,128]{1,0:T(8,128)(2,1)S(1)}) custom-call(bf16[16,16,128]{2,1,0:T(8,128)(2,1)S(1)} %shard_map.39.coef_half, bf16[16,16,128]{2,1,0:T(8,128)(2,1)S(1)} %collective-permute-done.7.coef_other, bf16[25,16,128]{2,1,0:T(8,128)(2,1)S(1)} %collective-permute-done.1.right_1, ...), custom_call_target="tpu_custom_call" | custom-call | flops 8000000 | bytes 800000 | tf_op jit(solution)/shard_map/pallas_call | solution.py:309
  48.2 0.0 collective-permute-done.2.right_2
  48.2 0.0 collective-permute-done.4.far_1
  48.2 2.5 %shard_map.42 = bf16[256,4096]{1,0:T(8,128)(2,1)} custom-call(s32[1,1024]{1,0:T(1,128)S(1)} %get-tuple-element.16.near, bf16[25,16,128]{2,1,0:T(8,128)(2,1)S(1)} %collective-permute-done.1.right_1, bf16[44,16,128]{2,1,0:T(8,128)(2,1)S(1)} %collective-permute-done.2.right_2, ...), custom_call_target="tpu_custom_call", output_to_operand_aliasing={{}: (7, {})} | custom-call | flops 3000000 | bytes 300000 | tf_op jit(solution)/shard_map/pallas_call | solution.py:317
  (4 shorter events, 0.0 us)
Async XLA Ops:
  0.0 4.4 %collective-permute-start = (bf16[32,2048]{1,0:T(8,128)(2,1)}, bf16[32,2048]{1,0:T(8,128)(2,1)S(1)}, u32[]{:S(2)}, u32[]{:S(2)}) collective-permute-start(bf16[32,2048]{1,0:T(8,128)(2,1)} %param.3), channel_id=1, source_target_pairs={{0,4},{4,0},{1,5},{5,1},{2,6},{6,2},{3,7},{7,3},{8,12},{12,8},{9,1... | collective-permute-start | bytes 393224 | tf_op jit(solution)/shard_map/ppermute | solution.py:269
  28.2 5.9 %collective-permute-start.3 = (bf16[49,16,128]{2,1,0:T(8,128)(2,1)S(1)}, bf16[49,16,128]{2,1,0:T(8,128)(2,1)S(1)}, u32[]{:S(2)}, u32[]{:S(2)}) collective-permute-start(bf16[49,16,128]{2,1,0:T(8,128)(2,1)S(1)} %get-tuple-element.21), channel_id=1, source_target_pairs={{0,1},{1,2},{2,3},{3,0},{4,5},{5,6},{6,7},{7,4},{8,9},{9,10},{10,1... | collective-permute-start | bytes 602120 | tf_op jit(solution)/shard_map/ppermute | solution.py:265
  29.5 7.9 %collective-permute-start.1 = (bf16[25,16,128]{2,1,0:T(8,128)(2,1)S(1)}, bf16[25,16,128]{2,1,0:T(8,128)(2,1)S(1)}, u32[]{:S(2)}, u32[]{:S(2)}) collective-permute-start(bf16[25,16,128]{2,1,0:T(8,128)(2,1)S(1)} %get-tuple-element.19), channel_id=1, source_target_pairs={{0,3},{1,0},{2,1},{3,2},{4,7},{5,4},{6,5},{7,6},{8,11},{9,8},{10,9... | collective-permute-start | bytes 307208 | tf_op jit(solution)/shard_map/ppermute | solution.py:265
  30.9 17.3 %collective-permute-start.2 = (bf16[44,16,128]{2,1,0:T(8,128)(2,1)S(1)}, bf16[44,16,128]{2,1,0:T(8,128)(2,1)S(1)}, u32[]{:S(2)}, u32[]{:S(2)}) collective-permute-start(bf16[44,16,128]{2,1,0:T(8,128)(2,1)S(1)} %get-tuple-element.20), channel_id=1, source_target_pairs={{0,3},{1,0},{2,1},{3,2},{4,7},{5,4},{6,5},{7,6},{8,11},{9,8},{10,9... | collective-permute-start | bytes 540680 | tf_op jit(solution)/shard_map/ppermute | solution.py:265
  34.0 14.2 %collective-permute-start.4 = (bf16[44,16,128]{2,1,0:T(8,128)(2,1)S(1)}, bf16[44,16,128]{2,1,0:T(8,128)(2,1)S(1)}, u32[]{:S(2)}, u32[]{:S(2)}) collective-permute-start(bf16[44,16,128]{2,1,0:T(8,128)(2,1)S(1)} %slice.8), channel_id=1, source_target_pairs={{0,1},{1,2},{2,3},{3,0},{4,5},{5,6},{6,7},{7,4},{8,9},{9,10},{10,1... | collective-permute-start | bytes 540680 | tf_op jit(solution)/shard_map/ppermute | solution.py:265
  34.1 5.9 %collective-permute-start.6 = (bf16[5,16,128]{2,1,0:T(8,128)(2,1)S(1)}, bf16[5,16,128]{2,1,0:T(8,128)(2,1)S(1)}, u32[]{:S(2)}, u32[]{:S(2)}) collective-permute-start(bf16[5,16,128]{2,1,0:T(8,128)(2,1)S(1)} %get-tuple-element.22), channel_id=1, source_target_pairs={{0,2},{1,3},{2,0},{3,1},{4,6},{5,7},{6,4},{7,5},{8,10},{9,11},{10,... | collective-permute-start | bytes 61448 | tf_op jit(solution)/shard_map/ppermute | solution.py:265
  36.6 8.2 %collective-permute-start.8 = (bf16[20,16,128]{2,1,0:T(8,128)(2,1)S(1)}, bf16[20,16,128]{2,1,0:T(8,128)(2,1)S(1)}, u32[]{:S(2)}, u32[]{:S(2)}) collective-permute-start(bf16[20,16,128]{2,1,0:T(8,128)(2,1)S(1)} %get-tuple-element.23), channel_id=1, source_target_pairs={{0,1},{1,2},{2,3},{3,0},{4,5},{5,6},{6,7},{7,4},{8,9},{9,10},{10,1... | collective-permute-start | bytes 245768 | tf_op jit(solution)/shard_map/ppermute | solution.py:265
  37.4 10.8 %collective-permute-start.5 = (bf16[20,16,128]{2,1,0:T(8,128)(2,1)S(1)}, bf16[20,16,128]{2,1,0:T(8,128)(2,1)S(1)}, u32[]{:S(2)}, u32[]{:S(2)}) collective-permute-start(bf16[20,16,128]{2,1,0:T(8,128)(2,1)S(1)} %slice.9), channel_id=1, source_target_pairs={{0,3},{1,0},{2,1},{3,2},{4,7},{5,4},{6,5},{7,6},{8,11},{9,8},{10,9... | collective-permute-start | bytes 245768 | tf_op jit(solution)/shard_map/ppermute | solution.py:265
  40.0 6.1 %collective-permute-start.7 = (bf16[16,16,128]{2,1,0:T(8,128)(2,1)S(1)}, bf16[16,16,128]{2,1,0:T(8,128)(2,1)S(1)}, u32[]{:S(2)}, u32[]{:S(2)}) collective-permute-start(bf16[16,16,128]{2,1,0:T(8,128)(2,1)S(1)} %shard_map.39.coef_half), channel_id=1, source_target_pairs={{0,4},{4,0},{1,5},{5,1},{2,6},{6,2},{3,7},{7,3},{8,12},{12,8},{9,1... | collective-permute-start | bytes 196616 | tf_op jit(solution)/shard_map/ppermute | solution.py:269
